TPU v7x, 32 devices: a whole 2x2x4 slice. The times are simulated.
32 devices in a mesh: gx: 4 (over z), gy: 8 (over y, x, core).
Axes of the slice: x: 2, y: 2, z: 4, core: 2. Of those that a mesh axis runs over, the one named last changes fastest.
Arguments:
- x_gen: bfloat16 [8, 512, 3072], P('gy', 'gx'), may hold values from -6 to 6
- fresh_noise: bfloat16 [8, 512, 3072], P('gy', 'gx'), may hold values from -6 to 6
- steps_t: int32 [8], P('gy'), may hold values from 0 to 999
- real_mod: float32 [8, 2, 3072], P('gy'), may hold values from -2.5 to 2.5
- real_w_up: bfloat16 [3072, 6144], P(None, 'gx'), may hold values from -0.109375 to 0.109375
- real_b_up: float32 [6144], P('gx'), may hold values from -3 to 3
- real_w_down: bfloat16 [6144, 3072], P('gx'), may hold values from -0.078125 to 0.078125
- fake_mod: float32 [8, 2, 3072], P('gy'), may hold values from -2.5 to 2.5
- fake_w_up: bfloat16 [3072, 6144], P('gy', 'gx'), may hold values from -0.109375 to 0.109375
- fake_b_up: float32 [6144], P('gx'), may hold values from -3 to 3
- fake_w_down: bfloat16 [6144, 3072], P('gx', 'gy'), may hold values from -0.078125 to 0.078125
Outputs:
- dmd_grad: float32 [8, 512, 3072], P('gy', 'gx')
- fake_grad: float32 [3072, 6144], P('gy', 'gx')
All inputs are finite; a program needn't handle non-finite values.
Results may differ from a plain program's by a relative error of at most 0.013.
Values may be sent and summed in bfloat16 or wider, within the bound.
A program may use at most 128 MiB of HBM per device.

v0:
```python
import jax
import jax.numpy as jnp
from jax import lax
from jax.sharding import PartitionSpec as P

TSTEPS = 1000


def layer_norm(values):
    center = values - jnp.mean(values, axis=-1, keepdims=True)
    spread = jnp.mean(center * center, axis=-1, keepdims=True)
    return center * lax.rsqrt(spread + 1e-06)


def modulate(normed, modulation):
    return (normed * (1.0 + modulation[1]) + modulation[0]).astype(jnp.bfloat16)


def shards(
    x_gen,
    fresh_noise,
    steps_t,
    real_mod,
    real_w_up,
    real_b_up,
    real_w_down,
    fake_mod,
    fake_w_up,
    fake_b_up,
    fake_w_down,
):
    noise_level = (steps_t[0].astype(jnp.float32) + 1.0) / TSTEPS
    clean_f = x_gen[0].astype(jnp.float32)
    drawn_f = fresh_noise[0].astype(jnp.float32)
    noised = ((1.0 - noise_level) * clean_f + noise_level * drawn_f).astype(jnp.bfloat16)
    target = (drawn_f - clean_f).astype(jnp.bfloat16)
    own_rows = noised.shape[0]
    noised_all = lax.all_gather(noised, "gx", axis=0, tiled=True)
    normed = layer_norm(noised_all.astype(jnp.float32))
    real_in = modulate(normed, real_mod[0])
    real_hidden = jax.nn.gelu(
        jnp.dot(real_in, real_w_up, preferred_element_type=jnp.float32) + real_b_up,
        approximate=True,
    ).astype(jnp.bfloat16)
    real_part = jnp.dot(real_hidden, real_w_down, preferred_element_type=jnp.float32)
    fake_in = modulate(normed, fake_mod[0])
    columns = fake_in
    fake_pre = jnp.dot(
        columns,
        lax.all_gather(fake_w_up, "gy", axis=0, tiled=True),
        preferred_element_type=jnp.float32,
    )
    fake_hidden = jax.nn.gelu(fake_pre + fake_b_up, approximate=True).astype(jnp.bfloat16)
    fake_part = jnp.dot(
        fake_hidden,
        lax.all_gather(fake_w_down, "gy", axis=1, tiled=True),
        preferred_element_type=jnp.float32,
    )
    real_rows, fake_rows = (
        lax.psum_scatter(
            real_part.astype(jnp.bfloat16), "gx", scatter_dimension=0, tiled=True
        ).astype(jnp.float32),
        lax.psum_scatter(
            fake_part.astype(jnp.bfloat16), "gx", scatter_dimension=0, tiled=True
        ).astype(jnp.float32),
    )
    error_v = (fake_rows - target.astype(jnp.float32)).astype(jnp.bfloat16)
    error_all = lax.all_gather(error_v, "gx", axis=0, tiled=True)
    dmd_grad = (fake_rows - real_rows)[None]
    loss_scale = float(lax.axis_size("gy") * lax.axis_size("gx") * own_rows) ** (-0.5)
    columns = error_all
    product = lax.dot_general(
        columns, fake_hidden, (((0,), (0,)), ((), ())), preferred_element_type=jnp.float32
    )
    fake_grad = lax.psum_scatter(
        (product * loss_scale).astype(jnp.bfloat16), "gy", scatter_dimension=0, tiled=True
    ).astype(jnp.float32)
    return (dmd_grad, fake_grad)


def solution(mesh):
    return jax.shard_map(
        shards,
        mesh=mesh,
        in_specs=(
            P("gy", "gx", None),
            P("gy", "gx", None),
            P("gy"),
            P("gy", None, None),
            P(None, "gx"),
            P("gx"),
            P("gx", None),
            P("gy", None, None),
            P("gy", "gx"),
            P("gx"),
            P("gx", "gy"),
        ),
        out_specs=(P("gy", "gx", None), P("gy", "gx")),
        check_vma=False,
    )
```

profile of v0, /device:TPU:0, one launch (start us, length us, event | category | flops | bytes accessed | tf_op | source)
XLA Modules:
  0.0 485.3 jit_solution(11168330511052977297)
XLA Ops:
  7.2 0.0 all-gather.12.cloned.1.call-start
  7.9 2.5 fusion.43
  10.4 0.0 all-gather.12.cloned.1.call-update
  10.4 0.0 all-gather.6.cloned.1.call-start
  10.5 0.7 all-gather.6.cloned.1.call-update
  11.2 0.0 all-gather.8.cloned.1.call-start
  11.2 0.7 all-gather.8.cloned.1.call-update
  11.9 0.0 reduce-scatter.6.cloned.1.call-start
  12.0 64.7 %all-gather.12.cloned.1.call-done = bf16[1,512,3072]{2,1,0:T(8,128)(2,1)} async-done(((bf16[1,128,3072]{2,1,0:T(8,128)(2,1)}), bf16[1,512,3072]{2,1,0:T(8,128)(2,1)}) %all-gather.12.cloned.1.call-update) | async-done | bytes 3145744 | tf_op jit(solution)/shard_map/all_gather | solution.py:38
  76.8 2.5 convert_reduce_fusion
  79.3 0.3 copy-done
  79.6 1.0 fusion.9
  80.6 19.8 %convolution_convert_fusion = bf16[512,3072]{1,0:T(8,128)(2,1)} fusion(bf16[1536,3072]{1,0:T(8,128)(2,1)} %param.17, bf16[3072,1536]{1,0:T(8,128)(2,1)} %param.15, bf16[1,512,3072]{2,1,0:T(8,128)(2,1)S(1)} %copy-done, f32[3072]{0:T(1024)S(1)} %bitcast.50, f32[3072]{0:T(1024)S(1)} %bitcast.49, f32[512]{0:T(512)S(1)} %add_rsqrt_fusion, ...), kind=kOutput, calls=%fused_computation.15 | convolution fusion | flops 9682550784 | bytes 25200640 | tf_op jit(solution)/shard_map/dot_general | solution.py:45
  100.3 0.0 reduce-scatter.6.cloned.1.call-update
  100.4 0.2 reduce-scatter.4.cloned.1.call-start
  100.6 0.5 copy-done.4
  101.1 34.9 %all-gather.6.cloned.1.call-done = bf16[3072,1536]{1,0:T(8,128)(2,1)} async-done(((bf16[384,1536]{1,0:T(8,128)(2,1)}), bf16[3072,1536]{1,0:T(8,128)(2,1)}) %all-gather.6.cloned.1.call-update) | async-done | bytes 9437200 | tf_op jit(solution)/shard_map/all_gather | solution.py:50
  136.0 10.5 %fusion.37 = bf16[512,1536]{1,0:T(8,128)(2,1)} fusion(bf16[3072,1536]{1,0:T(8,128)(2,1)} %all-gather.6.cloned.1.call-done, bf16[1,512,3072]{2,1,0:T(8,128)(2,1)S(1)} %copy-done, f32[3072]{0:T(1024)S(1)} %bitcast.52, f32[3072]{0:T(1024)S(1)} %bitcast.51, f32[512]{0:T(512)S(1)} %add_rsqrt_fusion, f32[512]{0:T(512)S(1)} %broadcast_multiply_fusion, ...), kind=kOutput, calls=%fused_computation.42 | convolution fusion | flops 4849139712 | bytes 14190592 | tf_op jit(solution)/shard_map/dot_general | solution.py:48
  146.5 51.9 %all-gather.8.cloned.1.call-done = bf16[1536,3072]{1,0:T(8,128)(2,1)} async-done(((bf16[1536,384]{1,0:T(8,128)(2,1)}), bf16[1536,3072]{1,0:T(8,128)(2,1)}) %all-gather.8.cloned.1.call-update) | async-done | bytes 9437200 | tf_op jit(solution)/shard_map/all_gather | solution.py:56
  198.4 9.2 %convolution_convert_fusion.1 = bf16[512,3072]{1,0:T(8,128)(2,1)} fusion(bf16[512,1536]{1,0:T(8,128)(2,1)} %fusion.37, bf16[1536,3072]{1,0:T(8,128)(2,1)} %all-gather.8.cloned.1.call-done), kind=kOutput, calls=%fused_computation.16 | convolution fusion | flops 4833411072 | bytes 14155776 | tf_op jit(solution)/shard_map/dot_general | solution.py:54
  207.7 0.0 reduce-scatter.4.cloned.1.call-update
  207.7 0.0 all-gather.10.cloned.1.call-start
  207.8 53.3 %reduce-scatter.6.cloned.1.call-done = bf16[128,3072]{1,0:T(8,128)(2,1)} async-done(((bf16[512,3072]{1,0:T(8,128)(2,1)}), bf16[128,3072]{1,0:T(8,128)(2,1)}) %reduce-scatter.6.cloned.1.call-update) | async-done | bytes 786448 | tf_op jit(solution)/shard_map/reduce_scatter | solution.py:60
  261.0 62.5 %reduce-scatter.4.cloned.1.call-done = bf16[128,3072]{1,0:T(8,128)(2,1)} async-done(((bf16[512,3072]{1,0:T(8,128)(2,1)}), bf16[128,3072]{1,0:T(8,128)(2,1)}) %reduce-scatter.4.cloned.1.call-update) | async-done | bytes 786448 | tf_op jit(solution)/shard_map/reduce_scatter | solution.py:63
  323.5 3.3 fusion.46
  326.8 0.0 all-gather.10.cloned.1.call-update
  326.8 0.0 reduce-scatter.8.cloned.1.call-start
  326.9 63.5 %all-gather.10.cloned.1.call-done = bf16[512,3072]{1,0:T(8,128)(2,1)} async-done(((bf16[128,3072]{1,0:T(8,128)(2,1)}), bf16[512,3072]{1,0:T(8,128)(2,1)}) %all-gather.10.cloned.1.call-update) | async-done | bytes 3145744 | tf_op jit(solution)/shard_map/all_gather | solution.py:68
  390.3 9.5 %multiply_convert_fusion = bf16[3072,1536]{1,0:T(8,128)(2,1)} fusion(bf16[512,3072]{1,0:T(8,128)(2,1)} %all-gather.10.cloned.1.call-done, bf16[512,1536]{1,0:T(8,128)(2,1)S(1)} %copy-done.7), kind=kOutput, calls=%fused_computation | convolution fusion | flops 4841275392 | bytes 14155776 | tf_op jit(solution)/shard_map/dot_general | solution.py:72
  399.9 0.0 reduce-scatter.8.cloned.1.call-update
  399.9 75.6 %reduce-scatter.8.cloned.1.call-done = bf16[384,1536]{1,0:T(8,128)(2,1)} async-done(((bf16[3072,1536]{1,0:T(8,128)(2,1)}), bf16[384,1536]{1,0:T(8,128)(2,1)}) %reduce-scatter.8.cloned.1.call-update) | async-done | bytes 1179664 | tf_op jit(solution)/shard_map/reduce_scatter | solution.py:75
  475.5 3.0 convert_element_type.83
  (18 shorter events, 0.1 us)
Async XLA Ops:
  7.2 4.8 copy-start.3
  7.2 69.6 %all-gather.12.cloned.1.call-start = ((), (), s32[]{:S(2)}) async-start(), calls=%async_computation.9 | async-start | bytes 3932160 | tf_op jit(solution)/shard_map/all_gather | solution.py:38
  10.4 125.6 %all-gather.6.cloned.1.call-start = ((), (), s32[]{:S(2)}) async-start(), calls=%async_computation.3 | async-start | bytes 10616832 | tf_op jit(solution)/shard_map/all_gather | solution.py:50
  11.2 187.2 %all-gather.8.cloned.1.call-start = ((), (), s32[]{:S(2)}) async-start(), calls=%async_computation.4 | async-start | bytes 10616832 | tf_op jit(solution)/shard_map/all_gather | solution.py:56
  11.9 249.1 %reduce-scatter.6.cloned.1.call-start = ((), (), s32[]{:S(2)}) async-start(), calls=%async_computation.6 | async-start | bytes 3932160 | tf_op jit(solution)/shard_map/reduce_scatter | solution.py:60
  76.8 2.8 copy-start
  76.8 3.8 copy-start.5
  100.3 0.7 copy-start.4
  100.3 35.7 %copy-start.6 = (f32[1536]{0:T(1024)S(1)}, f32[1536]{0:T(1024)}, u32[]{:S(2)}) copy-start(f32[1536]{0:T(1024)} %param.20) | copy-start | bytes 18436
  100.4 223.1 %reduce-scatter.4.cloned.1.call-start = ((), (), s32[]{:S(2)}) async-start(), calls=%async_computation.5 | async-start | bytes 3932160 | tf_op jit(solution)/shard_map/reduce_scatter | solution.py:63
  207.7 115.8 %copy-start.1 = (bf16[1,128,3072]{2,1,0:T(8,128)(2,1)S(1)}, bf16[1,128,3072]{2,1,0:T(8,128)(2,1)}, u32[]{:S(2)}) copy-start(bf16[1,128,3072]{2,1,0:T(8,128)(2,1)} %param.11) | copy-start | bytes 2359300
  207.7 115.8 %copy-start.2 = (bf16[1,128,3072]{2,1,0:T(8,128)(2,1)S(1)}, bf16[1,128,3072]{2,1,0:T(8,128)(2,1)}, u32[]{:S(2)}) copy-start(bf16[1,128,3072]{2,1,0:T(8,128)(2,1)} %param.12) | copy-start | bytes 2359300
  207.7 182.6 %copy-start.7 = (bf16[512,1536]{1,0:T(8,128)(2,1)S(1)}, bf16[512,1536]{1,0:T(8,128)(2,1)}, u32[]{:S(2)}) copy-start(bf16[512,1536]{1,0:T(8,128)(2,1)} %fusion.37) | copy-start | bytes 4718596
  207.7 182.6 %all-gather.10.cloned.1.call-start = ((), (), s32[]{:S(2)}) async-start(), calls=%async_computation.7 | async-start | bytes 3932160 | tf_op jit(solution)/shard_map/all_gather | solution.py:68
  326.8 148.7 %reduce-scatter.8.cloned.1.call-start = ((), (), s32[]{:S(2)}) async-start(), calls=%async_computation.8 | async-start | bytes 10616832 | tf_op jit(solution)/shard_map/reduce_scatter | solution.py:75
Sparse Core Ops, SparseCore 0:
  10.5 66.1 all-gather.11
  78.6 57.3 all-gather.5
  137.9 60.4 all-gather.7
  200.6 60.3 reduce-scatter.5
  263.2 60.3 reduce-scatter.3
  327.0 63.3 all-gather.9
  400.0 75.4 reduce-scatter.7
where the time goes:
time: 486 us; the launch traced here: 485 us
  waiting for transfers between devices  408 us (84%)
  matrix products  49 us (10%)
  between operations  14.8 us (3%)
  other arithmetic  12.3 us (3%)
    reduce_scatter x1, waiting for transfers between devices, shards(): lax.psum_scatter((product * loss_scale).astype(jnp.bfloat16), 'gy', scatt...  75.6 us
    all_gather x1, waiting for transfers between devices, shards(): noised_all = lax.all_gather(noised, 'gx', axis=0, tiled=True)  64.7 us
    all_gather x1, waiting for transfers between devices, shards(): error_all = lax.all_gather(error_v, 'gx', axis=0, tiled=True)  63.5 us
    reduce_scatter x1, waiting for transfers between devices, shards(): lax.psum_scatter(fake_part.astype(jnp.bfloat16), 'gx', scatter_dimension=...  62.5 us
    reduce_scatter x1, waiting for transfers between devices, shards(): lax.psum_scatter(real_part.astype(jnp.bfloat16), 'gx', scatter_dimension=...  53.3 us
    all_gather x1, waiting for transfers between devices, shards(): lax.all_gather(fake_w_down, 'gy', axis=1, tiled=True)  51.9 us
    all_gather x1, waiting for transfers between devices, shards(): lax.all_gather(fake_w_up, 'gy', axis=0, tiled=True)  34.9 us
    dot_general x1, matrix products, shards(): jnp.dot(real_hidden, real_w_down, preferred_element_type=jnp.float32)  19.8 us
  transfers between devices with their start and end apart: 7, of which 7 were waited for; matrix products, arithmetic and copies ran while one was open for 9% of the time, Pallas kernels for 0%

commit v1 on v0

--- a/solution.py
+++ b/solution.py
@@ -35,7 +35,12 @@
     noised = ((1.0 - noise_level) * clean_f + noise_level * drawn_f).astype(jnp.bfloat16)
     target = (drawn_f - clean_f).astype(jnp.bfloat16)
     own_rows = noised.shape[0]
-    noised_all = lax.all_gather(noised, "gx", axis=0, tiled=True)
+    ring = [noised]
+    for hop in range(3):
+        ring.append(lax.ppermute(ring[-1], "gx", [(dev, (dev + 1) % 4) for dev in range(4)]))
+    noised_all = jnp.roll(
+        jnp.concatenate(ring[::-1], axis=0), (lax.axis_index("gx") + 1) * ring[0].shape[0], axis=0
+    )
     normed = layer_norm(noised_all.astype(jnp.float32))
     real_in = modulate(normed, real_mod[0])
     real_hidden = jax.nn.gelu(

time: 486 us -> 383 us (0.79)
  waiting for transfers between devices: 408 us -> 299 us
    all_gather x1 -> x0, waiting for transfers between devices: 64.7 us -> none  [shards(): noised_all = lax.all_gather(noised, 'gx', axis=0, tiled=True)]
    ppermute x0 -> x3, waiting for transfers between devices: none -> 58.9 us  [shards(): lax.ppermute(ring[-1], 'gx', [(dev, (dev + 1) % 4) for dev in range(4)])]
    reduce_scatter x1, waiting for transfers between devices: 53.3 us -> 13.1 us  [shards(): lax.psum_scatter(real_part.astype(jnp.bfloat16), 'gx', scatter_dimension=...]
    all_gather x1, waiting for transfers between devices: 34.9 us -> 0.02 us  [shards(): lax.all_gather(fake_w_up, 'gy', axis=0, tiled=True)]
    all_gather x1, waiting for transfers between devices: 51.9 us -> 23.9 us  [shards(): lax.all_gather(fake_w_down, 'gy', axis=1, tiled=True)]
  transfers between devices with their start and end apart: 7 -> 9, of which waited for: 7 -> 8; matrix products, arithmetic and copies ran while one was open for 9% -> 12% of each run, Pallas kernels for 0% -> 0%
where the time goes in v1:
time: 383 us; the launch traced here: 382 us
  waiting for transfers between devices  299 us (78%)
  matrix products  51.1 us (13%)
  between operations  16.2 us (4%)
  other arithmetic  10.2 us (3%)
    reduce_scatter x1, waiting for transfers between devices, shards(): lax.psum_scatter((product * loss_scale).astype(jnp.bfloat16), 'gy', scatt...  75.6 us
    all_gather x1, waiting for transfers between devices, shards(): error_all = lax.all_gather(error_v, 'gx', axis=0, tiled=True)  63.2 us
    reduce_scatter x1, waiting for transfers between devices, shards(): lax.psum_scatter(fake_part.astype(jnp.bfloat16), 'gx', scatter_dimension=...  62.4 us
    ppermute x3, waiting for transfers between devices, shards(): lax.ppermute(ring[-1], 'gx', [(dev, (dev + 1) % 4) for dev in range(4)])  58.9 us
    all_gather x1, waiting for transfers between devices, shards(): lax.all_gather(fake_w_down, 'gy', axis=1, tiled=True)  23.9 us
    dot_general x1, matrix products, shards(): jnp.dot(real_hidden, real_w_down, preferred_element_type=jnp.float32)  20.7 us
    reduce_scatter x1, waiting for transfers between devices, shards(): lax.psum_scatter(real_part.astype(jnp.bfloat16), 'gx', scatter_dimension=...  13.1 us
    dot_general x1, matrix products, shards(): jnp.dot(columns, lax.all_gather(fake_w_up, 'gy', axis=0, tiled=True), pre...  10.8 us
  transfers between devices with their start and end apart: 9, of which 8 were waited for; matrix products, arithmetic and copies ran while one was open for 12% of the time, Pallas kernels for 0%

profile of v1, /device:TPU:0, one launch (start us, length us, event | category | flops | bytes accessed | tf_op | source)
XLA Modules:
  0.0 382.2 jit_solution(2764909385340322663)
XLA Ops:
  8.0 0.7 all-gather.4.cloned.1.call-update
  8.8 0.7 all-gather.6.cloned.1.call-update
  10.2 1.7 fusion.54
  11.8 3.1 collective-permute-start
  14.9 19.6 %collective-permute-done = bf16[128,3072]{1,0:T(8,128)(2,1)S(1)} collective-permute-done((bf16[128,3072]{1,0:T(8,128)(2,1)S(1)}, bf16[128,3072]{1,0:T(8,128)(2,1)S(1)}, u32[]{:S(2)}, u32[]{:S(2)}) %collective-permute-start) | collective-permute-done | bytes 786464 | tf_op jit(solution)/shard_map/ppermute | solution.py:40
  34.5 20.5 %collective-permute-done.1 = bf16[128,3072]{1,0:T(8,128)(2,1)S(1)} collective-permute-done((bf16[128,3072]{1,0:T(8,128)(2,1)S(1)}, bf16[128,3072]{1,0:T(8,128)(2,1)S(1)}, u32[]{:S(2)}, u32[]{:S(2)}) %collective-permute-start.1) | collective-permute-done | bytes 786464 | tf_op jit(solution)/shard_map/ppermute | solution.py:40
  55.0 0.8 slice_add_fusion
  55.9 18.8 %collective-permute-done.2 = bf16[128,3072]{1,0:T(8,128)(2,1)S(1)} collective-permute-done((bf16[128,3072]{1,0:T(8,128)(2,1)S(1)}, bf16[128,3072]{1,0:T(8,128)(2,1)S(1)}, u32[]{:S(2)}, u32[]{:S(2)}) %collective-permute-start.2) | collective-permute-done | bytes 786464 | tf_op jit(solution)/shard_map/ppermute | solution.py:40
  74.7 0.1 constant_dynamic-update-slice_fusion.7
  74.7 0.1 constant_dynamic-update-slice_fusion.6
  74.8 0.1 constant_dynamic-update-slice_fusion.5
  74.8 0.1 constant_dynamic-update-slice_fusion.4
  74.9 0.1 constant_dynamic-update-slice_fusion.3
  75.0 0.1 constant_dynamic-update-slice_fusion.2
  75.0 0.1 constant_dynamic-update-slice_fusion.1
  75.1 0.1 constant_dynamic-update-slice_fusion
  75.2 0.5 convert_reduce_fusion
  75.7 2.1 copy-done
  77.8 1.0 fusion.8
  78.7 20.7 %convolution_convert_fusion = bf16[512,3072]{1,0:T(8,128)(2,1)} fusion(bf16[1536,3072]{1,0:T(8,128)(2,1)} %param.17, bf16[3072,1536]{1,0:T(8,128)(2,1)} %param.15, f32[3072]{0:T(1024)S(1)} %bitcast.22, f32[3072]{0:T(1024)S(1)} %bitcast.21, f32[512]{0:T(512)S(1)} %add_rsqrt_fusion, f32[512]{0:T(512)S(1)} %broadcast_multiply_fusion, ...), kind=kOutput, calls=%fused_computation.14 | convolution fusion | flops 9682550784 | bytes 25200644 | tf_op jit(solution)/shard_map/dot_general | solution.py:50
  99.5 0.2 reduce-scatter.4.cloned.1.call-start
  99.8 10.8 %fusion.36 = bf16[512,1536]{1,0:T(8,128)(2,1)S(1)} fusion(bf16[3072,1536]{1,0:T(8,128)(2,1)} %all-gather.4.cloned.1.call-done, f32[3072]{0:T(1024)S(1)} %bitcast.24, f32[3072]{0:T(1024)S(1)} %bitcast.23, f32[512]{0:T(512)S(1)} %add_rsqrt_fusion, f32[512]{0:T(512)S(1)} %broadcast_multiply_fusion, bf16[1024,3072]{1,0:T(8,128)(2,1)} %copy-done, ...), kind=kOutput, calls=%fused_computation.41 | convolution fusion | flops 4849139712 | bytes 14190596 | tf_op jit(solution)/shard_map/dot_general | solution.py:53
  110.6 23.9 %all-gather.6.cloned.1.call-done = bf16[1536,3072]{1,0:T(8,128)(2,1)} async-done(((bf16[1536,384]{1,0:T(8,128)(2,1)}), bf16[1536,3072]{1,0:T(8,128)(2,1)}) %all-gather.6.cloned.1.call-update) | async-done | bytes 9437200 | tf_op jit(solution)/shard_map/all_gather | solution.py:61
  134.6 10.1 %convolution_convert_fusion.1 = bf16[512,3072]{1,0:T(8,128)(2,1)} fusion(bf16[512,1536]{1,0:T(8,128)(2,1)S(1)} %fusion.36, bf16[1536,3072]{1,0:T(8,128)(2,1)} %all-gather.6.cloned.1.call-done), kind=kOutput, calls=%fused_computation.15 | convolution fusion | flops 4833411072 | bytes 14155776 | tf_op jit(solution)/shard_map/dot_general | solution.py:59
  144.6 0.0 all-gather.8.cloned.1.call-start
  144.7 13.1 %reduce-scatter.6.cloned.1.call-done = bf16[128,3072]{1,0:T(8,128)(2,1)} async-done(((bf16[512,3072]{1,0:T(8,128)(2,1)}), bf16[128,3072]{1,0:T(8,128)(2,1)}) %reduce-scatter.6.cloned.1.call-update) | async-done | bytes 786448 | tf_op jit(solution)/shard_map/reduce_scatter | solution.py:65
  157.8 62.4 %reduce-scatter.4.cloned.1.call-done = bf16[128,3072]{1,0:T(8,128)(2,1)} async-done(((bf16[512,3072]{1,0:T(8,128)(2,1)}), bf16[128,3072]{1,0:T(8,128)(2,1)}) %reduce-scatter.4.cloned.1.call-update) | async-done | bytes 786448 | tf_op jit(solution)/shard_map/reduce_scatter | solution.py:68
  220.2 3.3 fusion.47
  223.6 63.2 %all-gather.8.cloned.1.call-done = bf16[512,3072]{1,0:T(8,128)(2,1)} async-done(((bf16[128,3072]{1,0:T(8,128)(2,1)}), bf16[512,3072]{1,0:T(8,128)(2,1)}) %all-gather.8.cloned.1.call-update) | async-done | bytes 3145744 | tf_op jit(solution)/shard_map/all_gather | solution.py:73
  286.8 9.5 %multiply_convert_fusion = bf16[3072,1536]{1,0:T(8,128)(2,1)} fusion(bf16[512,3072]{1,0:T(8,128)(2,1)} %all-gather.8.cloned.1.call-done, bf16[512,1536]{1,0:T(8,128)(2,1)S(1)} %fusion.36), kind=kOutput, calls=%fused_computation | convolution fusion | flops 4841275392 | bytes 14155776 | tf_op jit(solution)/shard_map/dot_general | solution.py:77
  296.3 75.6 %reduce-scatter.8.cloned.1.call-done = bf16[384,1536]{1,0:T(8,128)(2,1)} async-done(((bf16[3072,1536]{1,0:T(8,128)(2,1)}), bf16[384,1536]{1,0:T(8,128)(2,1)}) %reduce-scatter.8.cloned.1.call-update) | async-done | bytes 1179664 | tf_op jit(solution)/shard_map/reduce_scatter | solution.py:80
  371.9 3.0 convert_element_type.83
  (25 shorter events, 0.3 us)
Async XLA Ops:
  8.0 91.8 %all-gather.4.cloned.1.call-start = ((), (), s32[]{:S(2)}) async-start(), calls=%async_computation.3 | async-start | bytes 10616832 | tf_op jit(solution)/shard_map/all_gather | solution.py:55
  8.7 125.8 %all-gather.6.cloned.1.call-start = ((), (), s32[]{:S(2)}) async-start(), calls=%async_computation.4 | async-start | bytes 10616832 | tf_op jit(solution)/shard_map/all_gather | solution.py:61
  9.5 148.3 %reduce-scatter.6.cloned.1.call-start = ((), (), s32[]{:S(2)}) async-start(), calls=%async_computation.6 | async-start | bytes 3932160 | tf_op jit(solution)/shard_map/reduce_scatter | solution.py:65
  11.8 22.7 %collective-permute-start = (bf16[128,3072]{1,0:T(8,128)(2,1)S(1)}, bf16[128,3072]{1,0:T(8,128)(2,1)S(1)}, u32[]{:S(2)}, u32[]{:S(2)}) collective-permute-start(bf16[128,3072]{1,0:T(8,128)(2,1)S(1)} %fusion.54), channel_id=1, source_target_pairs={{0,8},{8,16},{16,24},{24,0},{1,9},{9,17},{17,25},{25,1},{2,10},{10... | collective-permute-start | bytes 2359304 | tf_op jit(solution)/shard_map/ppermute | solution.py:40
  34.5 20.5 %collective-permute-start.1 = (bf16[128,3072]{1,0:T(8,128)(2,1)S(1)}, bf16[128,3072]{1,0:T(8,128)(2,1)S(1)}, u32[]{:S(2)}, u32[]{:S(2)}) collective-permute-start(bf16[128,3072]{1,0:T(8,128)(2,1)S(1)} %collective-permute-done), channel_id=1, source_target_pairs={{0,8},{8,16},{16,24},{24,0},{1,9},{9,17},{17,25},{25,1},{2,10},{10... | collective-permute-start | bytes 2359304 | tf_op jit(solution)/shard_map/ppermute | solution.py:40
  55.0 19.6 %collective-permute-start.2 = (bf16[128,3072]{1,0:T(8,128)(2,1)S(1)}, bf16[128,3072]{1,0:T(8,128)(2,1)S(1)}, u32[]{:S(2)}, u32[]{:S(2)}) collective-permute-start(bf16[128,3072]{1,0:T(8,128)(2,1)S(1)} %collective-permute-done.1), channel_id=1, source_target_pairs={{0,8},{8,16},{16,24},{24,0},{1,9},{9,17},{17,25},{25,1},{2,10},{10... | collective-permute-start | bytes 2359304 | tf_op jit(solution)/shard_map/ppermute | solution.py:40
  74.9 3.8 copy-start.4
  75.2 2.6 copy-start
  78.7 21.0 %copy-start.3 = (f32[1,2,3072]{2,1,0:T(2,128)S(1)}, f32[1,2,3072]{2,1,0:T(2,128)}, u32[]{:S(2)}) copy-start(f32[1,2,3072]{2,1,0:T(2,128)} %param.18) | copy-start | bytes 73732
  78.7 21.1 %copy-start.5 = (f32[1536]{0:T(1024)S(1)}, f32[1536]{0:T(1024)}, u32[]{:S(2)}) copy-start(f32[1536]{0:T(1024)} %param.20) | copy-start | bytes 18436
  99.5 120.7 %reduce-scatter.4.cloned.1.call-start = ((), (), s32[]{:S(2)}) async-start(), calls=%async_computation.5 | async-start | bytes 3932160 | tf_op jit(solution)/shard_map/reduce_scatter | solution.py:68
  110.6 109.6 %copy-start.1 = (bf16[1,128,3072]{2,1,0:T(8,128)(2,1)S(1)}, bf16[1,128,3072]{2,1,0:T(8,128)(2,1)}, u32[]{:S(2)}) copy-start(bf16[1,128,3072]{2,1,0:T(8,128)(2,1)} %param.12) | copy-start | bytes 2359300
  110.6 109.6 %copy-start.2 = (bf16[1,128,3072]{2,1,0:T(8,128)(2,1)S(1)}, bf16[1,128,3072]{2,1,0:T(8,128)(2,1)}, u32[]{:S(2)}) copy-start(bf16[1,128,3072]{2,1,0:T(8,128)(2,1)} %param.11) | copy-start | bytes 2359300
  144.6 142.1 %all-gather.8.cloned.1.call-start = ((), (), s32[]{:S(2)}) async-start(), calls=%async_computation.7 | async-start | bytes 3932160 | tf_op jit(solution)/shard_map/all_gather | solution.py:73
  223.5 148.4 %reduce-scatter.8.cloned.1.call-start = ((), (), s32[]{:S(2)}) async-start(), calls=%async_computation.8 | async-start | bytes 10616832 | tf_op jit(solution)/shard_map/reduce_scatter | solution.py:80
Sparse Core Ops, SparseCore 0:
  10.7 61.4 all-gather.3
  74.0 60.5 all-gather.5
  296.4 75.4 reduce-scatter.7
Sparse Core Ops, SparseCore 1:
  99.6 58.1 reduce-scatter.5
  159.9 60.2 reduce-scatter.3
  223.6 63.1 all-gather.7
